TPU v7x, 32 devices: a whole 2x2x4 slice. The times are simulated.
32 devices in a mesh: seq: 4 (over x, core), ctx: 4 (over z), head: 2 (over y).
Axes of the slice: x: 2, y: 2, z: 4, core: 2. Of those that a mesh axis runs over, the one named last changes fastest.
Arguments:
- stream: bfloat16 [4, 256, 2880], P('seq', 'ctx'), may hold values from -6 to 6
- query_weight: bfloat16 [2880, 4096], P(None, 'head'), may hold values from -0.109375 to 0.109375
- cache_keys: bfloat16 [4, 8192, 8, 64], P('seq', 'ctx', 'head'), may hold values from -1000 to 1000
- cache_values: bfloat16 [4, 8192, 8, 64], P('seq', 'ctx', 'head'), may hold values from -6 to 6
- new_keys: bfloat16 [4, 256, 8, 64], P('seq', 'ctx', 'head'), may hold values from -18 to 18
- new_values: bfloat16 [4, 256, 8, 64], P('seq', 'ctx', 'head'), may hold values from -6 to 6
- out_weight: bfloat16 [4096, 2880], P('head'), may hold values from -0.09375 to 0.09375
- norm_gain: float32 [2880], replicated, may hold values from 0.5 to 1.5
- expert_ids: int32 [4, 256, 4], P('seq', 'ctx'), may hold values from 0 to 15, all different within a row; in each aligned block of 64 rows (0 to 63, 64 to 127, ..., all dimensions but the last counted through in order) at most 16 rows name the same one
- expert_weights: float32 [4, 256, 4], P('seq', 'ctx'), may hold values from 0.1 to 1
- gate_weight: bfloat16 [16, 2880, 2880], P(('seq', 'ctx'), None, 'head'), may hold values from -0.109375 to 0.109375
- up_weight: bfloat16 [16, 2880, 2880], P(('seq', 'ctx'), None, 'head'), may hold values from -0.109375 to 0.109375
- down_weight: bfloat16 [16, 2880, 2880], P(('seq', 'ctx'), 'head'), may hold values from -0.109375 to 0.109375
Outputs:
- mixed: bfloat16 [4, 256, 2880], P('seq', 'ctx', 'head')
Inputs may be any that keep to these rules, and one draw needn't show every extreme that they name: `expert_ids`: in each aligned block of 64 rows (the tokens of one device) no expert is named by more than 16 rows; each row names 4 different experts.
All inputs are finite; a program needn't handle non-finite values.
Results may differ from a plain program's by a relative error of at most 0.015.
Values may be sent and summed in bfloat16 or wider, within the bound.
No kernel may reach another device: no remote copies, remote signals or barrier semaphores. Data moves between devices by JAX's collectives and lax.ppermute only.
A program may use at most 128 MiB of HBM per device.

v0:
```python
import math
import jax
import jax.numpy as jnp
from jax import lax
from jax.sharding import PartitionSpec as P

CAP = 16


def passed_along(block, axis, distance):
    devices = range(lax.axis_size(axis))
    route = [((i - distance) % len(devices), i) for i in devices]
    return lax.ppermute(block, axis, route)


def body(
    stream,
    query_weight,
    cache_keys,
    cache_values,
    new_keys,
    new_values,
    out_weight,
    norm_gain,
    expert_ids,
    expert_weights,
    gate_weight,
    up_weight,
    down_weight,
):
    tokens = stream[0]
    count = tokens.shape[0]
    model = tokens.shape[1]
    kv_local = cache_keys.shape[2]
    head_dim = cache_keys.shape[3]
    group = query_weight.shape[1] // (kv_local * head_dim)
    cache_len = cache_keys.shape[1]
    height = count * group
    cycles = lax.axis_size("ctx")
    place = lax.axis_index("ctx")
    scale = 1.0 / math.sqrt(head_dim)
    query = jnp.dot(tokens, query_weight, preferred_element_type=jnp.float32).astype(jnp.bfloat16)
    query = (
        query.reshape(count, kv_local, group, head_dim)
        .transpose(1, 0, 2, 3)
        .reshape(kv_local, height, head_dim)
    )
    keys = jnp.concatenate([cache_keys[0], new_keys[0]], axis=0).transpose(1, 0, 2)
    values = jnp.concatenate([cache_values[0], new_values[0]], axis=0).transpose(1, 0, 2)
    extent = keys.shape[1]
    key_index = lax.broadcasted_iota(jnp.int32, (height, extent), 1)
    tok_index = lax.broadcasted_iota(jnp.int32, (height, extent), 0) // group
    fresh = key_index - cache_len
    blank = (
        jnp.full((kv_local, height), -jnp.inf, jnp.float32),
        jnp.zeros((kv_local, height), jnp.float32),
        jnp.zeros((kv_local, height, head_dim), jnp.float32),
    )

    def absorb(block, state, sources):
        top, total, numerator = state
        anchor = sources[:, None]
        allowed = (
            (key_index < cache_len) | (place < anchor) | (place == anchor) & (fresh <= tok_index)
        )
        scores = jnp.einsum("hrd,hkd->hrk", block, keys, preferred_element_type=jnp.float32) * scale
        scores = jnp.where(allowed[None], scores, -jnp.inf)
        new_top = jnp.maximum(top, jnp.max(scores, axis=-1))
        weights = jnp.exp(scores - new_top[..., None])
        fade = jnp.exp(top - new_top)
        total = total * fade + jnp.sum(weights, axis=-1)
        numerator = numerator * fade[..., None] + jnp.einsum(
            "hrk,hkd->hrd", weights.astype(jnp.bfloat16), values, preferred_element_type=jnp.float32
        )
        return (new_top, total, numerator)

    def turn(step, carry):
        sources = jnp.full((height,), (place - step) % cycles, jnp.int32)
        state = absorb(carry[0].astype(jnp.bfloat16), carry[1:], sources)
        return passed_along((carry[0],) + state, "ctx", 1)

    final = lax.fori_loop(0, cycles, turn, (query.astype(jnp.float32),) + blank)
    top, total, numerator = (final[1], final[2], final[3])
    attn = (numerator / total[..., None]).astype(jnp.bfloat16)
    attn = (
        attn.reshape(kv_local, count, group, head_dim)
        .transpose(1, 0, 2, 3)
        .reshape(count, kv_local * group * head_dim)
    )
    projected = jnp.dot(attn, out_weight, preferred_element_type=jnp.float32)
    width = model // lax.axis_size("head")
    offset = lax.axis_index("head") * width
    resid = tokens.astype(jnp.float32) + lax.psum(projected.astype(jnp.bfloat16), "head").astype(
        jnp.float32
    )
    normed = (
        resid * lax.rsqrt(jnp.mean(resid * resid, axis=-1, keepdims=True) + 1e-05) * norm_gain
    ).astype(jnp.bfloat16)
    resid_own = lax.dynamic_slice_in_dim(resid, offset, width, 1)
    experts = lax.axis_size("seq") * lax.axis_size("ctx")
    slots = experts * CAP
    chosen = expert_ids[0].reshape(-1)
    onehot = (chosen[:, None] == lax.broadcasted_iota(jnp.int32, (1, experts), 1)).astype(jnp.int32)
    before = jnp.cumsum(onehot, axis=0) - onehot
    target = chosen * CAP + jnp.sum(before * onehot, axis=1)
    matches = target[None, :] == lax.broadcasted_iota(jnp.int32, (slots, 1), 0)
    select = jnp.sum(matches.astype(jnp.float32).reshape(slots, count, -1), axis=-1).astype(
        jnp.bfloat16
    )
    packed = jnp.dot(select, normed, preferred_element_type=jnp.float32).astype(jnp.bfloat16)
    packed = packed.reshape(experts, CAP, normed.shape[1])
    arrived = lax.all_to_all(packed, ("seq", "ctx"), split_axis=0, concat_axis=0, tiled=True)
    rows = arrived.reshape(slots, normed.shape[1])
    gate = jnp.dot(rows, gate_weight[0], preferred_element_type=jnp.float32)
    up = jnp.dot(rows, up_weight[0], preferred_element_type=jnp.float32)
    hidden = (gate * jax.nn.sigmoid(1.702 * gate) * (up + 1.0)).astype(jnp.bfloat16)
    columns = down_weight[0]
    expert_out = lax.psum_scatter(
        jnp.einsum("fd,rf->dr", columns, hidden, preferred_element_type=jnp.float32).astype(
            jnp.bfloat16
        ),
        "head",
        scatter_dimension=0,
        tiled=True,
    )
    returned = lax.all_to_all(expert_out, ("seq", "ctx"), split_axis=1, concat_axis=1, tiled=True)
    spread_weights = jnp.where(matches.T, expert_weights[0].reshape(-1)[:, None], 0.0)
    spread_weights = jnp.sum(spread_weights.reshape(count, -1, slots), axis=1)
    moe = lax.dot_general(
        spread_weights,
        returned.astype(jnp.float32),
        (((1,), (1,)), ((), ())),
        precision=lax.Precision.HIGHEST,
    )
    return (resid_own + moe).astype(jnp.bfloat16)[None]


def solution(mesh):
    in_specs = (
        P("seq", "ctx", None),
        P(None, "head"),
        P("seq", "ctx", "head", None),
        P("seq", "ctx", "head", None),
        P("seq", "ctx", "head", None),
        P("seq", "ctx", "head", None),
        P("head", None),
        P(),
        P("seq", "ctx", None),
        P("seq", "ctx", None),
        P(("seq", "ctx"), None, "head"),
        P(("seq", "ctx"), None, "head"),
        P(("seq", "ctx"), "head", None),
    )
    out_specs = P("seq", "ctx", "head")
    return jax.shard_map(body, mesh=mesh, in_specs=in_specs, out_specs=out_specs, check_vma=False)
```

profile of v0, /device:TPU:0, one launch (start us, length us, event | category | flops | bytes accessed | tf_op | source)
XLA Modules:
  0.0 386.5 jit_solution(13312295736175083786)
XLA Ops:
  6.6 0.9 copy.34
  7.5 0.9 copy.35
  8.5 6.7 %fusion.43 = bf16[64,2048]{1,0:T(8,128)(2,1)S(1)} fusion(bf16[2880,2048]{1,0:T(8,128)(2,1)} %param.16, bf16[1,64,2880]{2,1,0:T(8,128)(2,1)} %param.15), kind=kOutput, calls=%fused_computation.38 | convolution fusion | flops 755105792 | bytes 12427264 | tf_op jit(solution)/shard_map/dot_general | solution.py:42
  16.4 2.4 maximum_bitcast_fusion
  18.9 205.2 %while.22 = (s32[]{:T(128)}, bf16[4,512,64]{1,2,0:T(8,128)(2,1)S(1)}, f32[4,512]{1,0:T(4,128)S(1)}, f32[4,512]{1,0:T(4,128)S(1)}, f32[4,512,64]{1,2,0:T(8,128)S(...) while((s32[]{:T(128)}, ...), condition=%wide.region_3.4_spmd.clone, body=%wide.region_0.3_spmd.clone.sunk | while | flops 1161629696 | bytes 63567040 | solution.py:82
  19.1 1.3 fusion.86
  20.5 7.7 %fusion.87 = (f32[4,512]{1,0:T(4,128)S(1)}, f32[4,512,2112]{1,2,0:T(8,128)}) fusion(pred[512,2112]{0,1:T(8,128)(4,1)S(1)} %fusion.86, bf16[4,512,64]{1,2,0:T(8,128)(2,1)S(1)} %copy.57, bf16[4,2112,64]{1,2,0:T(8,128)(2,1)S(1)} %get-tuple-element.480), kind=kOutput, calls=%fused_computation.4.clone.1 | convolution fusion | flops 566622208 | bytes 19734528 | tf_op jit(solution)/shard_map/while/body/eval_jaxpr/hrd,hkd->hrk/dot_general | solution.py:66
  28.2 9.6 %fusion.88 = f32[4,512]{1,0:T(4,128)S(1)} fusion(f32[4,512,2112]{1,2,0:T(8,128)} %get-tuple-element.439, f32[4,512]{1,0:T(4,128)S(1)} %max.12, pred[512,2112]{0,1:T(8,128)(4,1)S(1)} %fusion.86), kind=kLoop, calls=%fused_computation.6.clone.1 | loop fusion | flops 17299456 | bytes 18399232 | tf_op jit(solution)/shard_map/while/body/eval_jaxpr/reduce_sum | solution.py:71
  37.8 11.6 %fusion.89 = f32[4,512,64]{1,2,0:T(8,128)} fusion(bf16[4,2112,64]{1,2,0:T(8,128)(2,1)} %get-tuple-element.481, f32[4,512,2112]{1,2,0:T(8,128)} %get-tuple-element.439, f32[4,512]{1,0:T(4,128)S(1)} %max.12, pred[512,2112]{0,1:T(8,128)(4,1)S(1)} %fusion.86, f32[4,512,64]{1,2,0:T(8,128)S(1)} %get-tuple-element.462, f32[4,512]{1,0:T(4,128)S(1)} %get-tuple-element.441), kind=kOutput, calls=%fused_computation.15.clone.1 | convolution fusion | flops 571211776 | bytes 20529152 | tf_op jit(solution)/shard_map/while/body/eval_jaxpr/hrk,hkd->hrd/dot_general | solution.py:72
  49.4 3.1 collective-permute-start.3
  52.4 1.6 collective-permute-start
  54.0 1.6 collective-permute-start.1
  55.6 16.9 %collective-permute-done.1 = f32[4,512]{1,0:T(4,128)S(1)} collective-permute-done((f32[4,512]{1,0:T(4,128)S(1)}, f32[4,512]{1,0:T(4,128)S(1)}, u32[]{:S(2)}, u32[]{:S(2)}) %collective-permute-start.1) | collective-permute-done | bytes 8224 | tf_op jit(solution)/shard_map/while/body/eval_jaxpr/ppermute | solution.py:13
  72.6 1.3 fusion.86
  73.9 7.7 %fusion.87 = (f32[4,512]{1,0:T(4,128)S(1)}, f32[4,512,2112]{1,2,0:T(8,128)}) fusion(pred[512,2112]{0,1:T(8,128)(4,1)S(1)} %fusion.86, bf16[4,512,64]{1,2,0:T(8,128)(2,1)S(1)} %copy.57, bf16[4,2112,64]{1,2,0:T(8,128)(2,1)S(1)} %get-tuple-element.480), kind=kOutput, calls=%fused_computation.4.clone.1 | convolution fusion | flops 566622208 | bytes 19734528 | tf_op jit(solution)/shard_map/while/body/eval_jaxpr/hrd,hkd->hrk/dot_general | solution.py:66
  81.6 9.6 %fusion.88 = f32[4,512]{1,0:T(4,128)S(1)} fusion(f32[4,512,2112]{1,2,0:T(8,128)} %get-tuple-element.439, f32[4,512]{1,0:T(4,128)S(1)} %max.12, pred[512,2112]{0,1:T(8,128)(4,1)S(1)} %fusion.86), kind=kLoop, calls=%fused_computation.6.clone.1 | loop fusion | flops 17299456 | bytes 18399232 | tf_op jit(solution)/shard_map/while/body/eval_jaxpr/reduce_sum | solution.py:71
  91.2 11.6 %fusion.89 = f32[4,512,64]{1,2,0:T(8,128)} fusion(bf16[4,2112,64]{1,2,0:T(8,128)(2,1)} %get-tuple-element.481, f32[4,512,2112]{1,2,0:T(8,128)} %get-tuple-element.439, f32[4,512]{1,0:T(4,128)S(1)} %max.12, pred[512,2112]{0,1:T(8,128)(4,1)S(1)} %fusion.86, f32[4,512,64]{1,2,0:T(8,128)S(1)} %get-tuple-element.462, f32[4,512]{1,0:T(4,128)S(1)} %get-tuple-element.441), kind=kOutput, calls=%fused_computation.15.clone.1 | convolution fusion | flops 571211776 | bytes 20529152 | tf_op jit(solution)/shard_map/while/body/eval_jaxpr/hrk,hkd->hrd/dot_general | solution.py:72
  102.8 1.3 collective-permute-start
  104.1 1.6 collective-permute-start.1
  105.7 2.1 collective-permute-start.2
  107.8 16.0 %collective-permute-done.1 = f32[4,512]{1,0:T(4,128)S(1)} collective-permute-done((f32[4,512]{1,0:T(4,128)S(1)}, f32[4,512]{1,0:T(4,128)S(1)}, u32[]{:S(2)}, u32[]{:S(2)}) %collective-permute-start.1) | collective-permute-done | bytes 8224 | tf_op jit(solution)/shard_map/while/body/eval_jaxpr/ppermute | solution.py:13
  123.9 1.3 fusion.86
  125.2 7.7 %fusion.87 = (f32[4,512]{1,0:T(4,128)S(1)}, f32[4,512,2112]{1,2,0:T(8,128)}) fusion(pred[512,2112]{0,1:T(8,128)(4,1)S(1)} %fusion.86, bf16[4,512,64]{1,2,0:T(8,128)(2,1)S(1)} %copy.57, bf16[4,2112,64]{1,2,0:T(8,128)(2,1)S(1)} %get-tuple-element.480), kind=kOutput, calls=%fused_computation.4.clone.1 | convolution fusion | flops 566622208 | bytes 19734528 | tf_op jit(solution)/shard_map/while/body/eval_jaxpr/hrd,hkd->hrk/dot_general | solution.py:66
  133.0 9.6 %fusion.88 = f32[4,512]{1,0:T(4,128)S(1)} fusion(f32[4,512,2112]{1,2,0:T(8,128)} %get-tuple-element.439, f32[4,512]{1,0:T(4,128)S(1)} %max.12, pred[512,2112]{0,1:T(8,128)(4,1)S(1)} %fusion.86), kind=kLoop, calls=%fused_computation.6.clone.1 | loop fusion | flops 17299456 | bytes 18399232 | tf_op jit(solution)/shard_map/while/body/eval_jaxpr/reduce_sum | solution.py:71
  142.5 11.6 %fusion.89 = f32[4,512,64]{1,2,0:T(8,128)} fusion(bf16[4,2112,64]{1,2,0:T(8,128)(2,1)} %get-tuple-element.481, f32[4,512,2112]{1,2,0:T(8,128)} %get-tuple-element.439, f32[4,512]{1,0:T(4,128)S(1)} %max.12, pred[512,2112]{0,1:T(8,128)(4,1)S(1)} %fusion.86, f32[4,512,64]{1,2,0:T(8,128)S(1)} %get-tuple-element.462, f32[4,512]{1,0:T(4,128)S(1)} %get-tuple-element.441), kind=kOutput, calls=%fused_computation.15.clone.1 | convolution fusion | flops 571211776 | bytes 20529152 | tf_op jit(solution)/shard_map/while/body/eval_jaxpr/hrk,hkd->hrd/dot_general | solution.py:72
  154.1 0.8 collective-permute-start.1
  154.9 4.2 %collective-permute-start.2 = (f32[4,512]{1,0:T(4,128)S(1)}, f32[4,512]{1,0:T(4,128)S(1)}, u32[]{:S(2)}, u32[]{:S(2)}) collective-permute-start(f32[4,512]{1,0:T(4,128)S(1)} %get-tuple-element.440), channel_id=1, source_target_pairs={{6,0},{0,2},{2,4},{4,6},{7,1},{1,3},{3,5},{5,7},{14,8},{8,10},{10,... | collective-permute-start | bytes 24584 | tf_op jit(solution)/shard_map/while/body/eval_jaxpr/ppermute | solution.py:13
  159.1 15.2 %collective-permute-done.1 = f32[4,512]{1,0:T(4,128)S(1)} collective-permute-done((f32[4,512]{1,0:T(4,128)S(1)}, f32[4,512]{1,0:T(4,128)S(1)}, u32[]{:S(2)}, u32[]{:S(2)}) %collective-permute-start.1) | collective-permute-done | bytes 8224 | tf_op jit(solution)/shard_map/while/body/eval_jaxpr/ppermute | solution.py:13
  174.4 1.3 fusion.86
  175.7 7.7 %fusion.87 = (f32[4,512]{1,0:T(4,128)S(1)}, f32[4,512,2112]{1,2,0:T(8,128)}) fusion(pred[512,2112]{0,1:T(8,128)(4,1)S(1)} %fusion.86, bf16[4,512,64]{1,2,0:T(8,128)(2,1)S(1)} %copy.57, bf16[4,2112,64]{1,2,0:T(8,128)(2,1)S(1)} %get-tuple-element.480), kind=kOutput, calls=%fused_computation.4.clone.1 | convolution fusion | flops 566622208 | bytes 19734528 | tf_op jit(solution)/shard_map/while/body/eval_jaxpr/hrd,hkd->hrk/dot_general | solution.py:66
  183.4 9.6 %fusion.88 = f32[4,512]{1,0:T(4,128)S(1)} fusion(f32[4,512,2112]{1,2,0:T(8,128)} %get-tuple-element.439, f32[4,512]{1,0:T(4,128)S(1)} %max.12, pred[512,2112]{0,1:T(8,128)(4,1)S(1)} %fusion.86), kind=kLoop, calls=%fused_computation.6.clone.1 | loop fusion | flops 17299456 | bytes 18399232 | tf_op jit(solution)/shard_map/while/body/eval_jaxpr/reduce_sum | solution.py:71
  193.0 11.6 %fusion.89 = f32[4,512,64]{1,2,0:T(8,128)} fusion(bf16[4,2112,64]{1,2,0:T(8,128)(2,1)} %get-tuple-element.481, f32[4,512,2112]{1,2,0:T(8,128)} %get-tuple-element.439, f32[4,512]{1,0:T(4,128)S(1)} %max.12, pred[512,2112]{0,1:T(8,128)(4,1)S(1)} %fusion.86, f32[4,512,64]{1,2,0:T(8,128)S(1)} %get-tuple-element.462, f32[4,512]{1,0:T(4,128)S(1)} %get-tuple-element.441), kind=kOutput, calls=%fused_computation.15.clone.1 | convolution fusion | flops 571211776 | bytes 20529152 | tf_op jit(solution)/shard_map/while/body/eval_jaxpr/hrk,hkd->hrd/dot_general | solution.py:72
  204.6 0.7 collective-permute-start.1
  205.3 4.3 %collective-permute-start.2 = (f32[4,512]{1,0:T(4,128)S(1)}, f32[4,512]{1,0:T(4,128)S(1)}, u32[]{:S(2)}, u32[]{:S(2)}) collective-permute-start(f32[4,512]{1,0:T(4,128)S(1)} %get-tuple-element.440), channel_id=1, source_target_pairs={{6,0},{0,2},{2,4},{4,6},{7,1},{1,3},{3,5},{5,7},{14,8},{8,10},{10,... | collective-permute-start | bytes 24584 | tf_op jit(solution)/shard_map/while/body/eval_jaxpr/ppermute | solution.py:13
  209.5 14.3 %collective-permute-done.1 = f32[4,512]{1,0:T(4,128)S(1)} collective-permute-done((f32[4,512]{1,0:T(4,128)S(1)}, f32[4,512]{1,0:T(4,128)S(1)}, u32[]{:S(2)}, u32[]{:S(2)}) %collective-permute-start.1) | collective-permute-done | bytes 8224 | tf_op jit(solution)/shard_map/while/body/eval_jaxpr/ppermute | solution.py:13
  225.4 8.8 %convolution_convert_fusion.1 = bf16[64,2880]{1,0:T(8,128)(2,1)} fusion(bf16[64,2048]{1,0:T(8,128)(2,1)S(1)} %reshape.172, bf16[2048,2880]{0,1:T(8,128)(2,1)} %param.21), kind=kOutput, calls=%fused_computation.31 | convolution fusion | flops 755159040 | bytes 12427264 | tf_op jit(solution)/shard_map/dot_general | solution.py:90
  235.8 21.4 %all-reduce.2.cloned.1.call-done = bf16[64,2880]{1,0:T(8,128)(2,1)} async-done(((bf16[64,2880]{1,0:T(8,128)(2,1)}), bf16[64,2880]{1,0:T(8,128)(2,1)}) %all-reduce.2.cloned.1.call-update) | async-done | bytes 368656 | tf_op jit(solution)/shard_map/psum | solution.py:93
  257.3 2.1 convert_add_fusion
  259.4 1.7 convolution_convert_fusion
  261.1 1.0 copy.45
  262.1 42.1 %all_to_all.17 = bf16[16,16,2880]{2,1,0:T(8,128)(2,1)S(1)} all-to-all(bf16[16,16,2880]{2,1,0:T(8,128)(2,1)S(1)} %bitcast.102), channel_id=1, replica_groups=mesh['seq'=4,'ctx'=4,'head'=2] {'seq','ctx'}, dimensions={0} | all-to-all | bytes 2949120 | tf_op jit(solution)/shard_map/all_to_all | solution.py:112
  304.1 5.9 %fusion.25 = f32[256,1440]{0,1:T(8,128)S(1)} fusion(bf16[256,2880]{1,0:T(8,128)(2,1)S(1)} %bitcast.105, bf16[1,2880,1440]{1,2,0:T(8,128)(2,1)} %param.25), kind=kOutput, calls=%fused_computation.26 | convolution fusion | flops 2123366400 | bytes 11243520 | tf_op jit(solution)/shard_map/dot_general | solution.py:114
  310.0 16.2 %fusion.30 = bf16[2880,256]{1,0:T(8,128)(2,1)} fusion(bf16[1,1440,2880]{2,1,0:T(8,128)(2,1)} %param.27, bf16[256,2880]{1,0:T(8,128)(2,1)S(1)} %bitcast.106, bf16[1,2880,1440]{1,2,0:T(8,128)(2,1)} %param.26, f32[256,1440]{0,1:T(8,128)S(1)} %fusion.25), kind=kOutput, calls=%fused_computation.30 | convolution fusion | flops 4250419200 | bytes 21012480 | tf_op jit(solution)/shard_map/fd,rf->dr/dot_general | solution.py:119
  326.3 23.0 %reduce-scatter.2.cloned.1.call-done = bf16[1440,256]{1,0:T(8,128)(2,1)} async-done(((bf16[2880,256]{1,0:T(8,128)(2,1)}), bf16[1440,256]{1,0:T(8,128)(2,1)}) %reduce-scatter.2.cloned.1.call-update) | async-done | bytes 737296 | tf_op jit(solution)/shard_map/reduce_scatter | solution.py:118
  349.3 2.3 copy.46
  351.6 5.6 %all-to-all-start.1 = ((bf16[1440,16,16]{0,2,1:T(8,128)(2,1)}), bf16[1440,16,16]{0,2,1:T(8,128)(2,1)S(1)}, u32[]{:S(2)}, u32[]{:S(2)}) async-start(bf16[1440,16,16]{0,2,1:T(8,128)(2,1)} %bitcast.20), calls=%async_computation.2 | async-start | bytes 1572864 | tf_op jit(solution)/shard_map/all_to_all | solution.py:126
  357.4 21.1 %all-to-all-done.1 = bf16[1440,16,16]{0,2,1:T(8,128)(2,1)S(1)} async-done(((bf16[1440,16,16]{0,2,1:T(8,128)(2,1)}), bf16[1440,16,16]{0,2,1:T(8,128)(2,1)S(1)}, u32[]{:S(2)}, u32[]{:S(2)}) %all-to-all-start.1) | async-done | bytes 737312 | tf_op jit(solution)/shard_map/all_to_all | solution.py:126
  378.4 1.2 fusion.44
  (74 shorter events, 4.8 us)
Async XLA Ops:
  6.5 250.7 %all-reduce.2.cloned.1.call-start = ((), (), s32[]{:S(2)}) async-start(), calls=%async_computation.3 | async-start | bytes 753664 | tf_op jit(solution)/shard_map/psum | solution.py:93
  15.2 1.2 copy-start.2
  49.4 23.2 %collective-permute-start.3 = (f32[4,512,64]{1,2,0:T(8,128)}, f32[4,512,64]{1,2,0:T(8,128)S(1)}, u32[]{:S(2)}, u32[]{:S(2)}) collective-permute-start(f32[4,512,64]{1,2,0:T(8,128)} %fusion.89), channel_id=1, source_target_pairs={{6,0},{0,2},{2,4},{4,6},{7,1},{1,3},{3,5},{5,7},{14,8},{8,10},{10,... | collective-permute-start | bytes 1572872 | tf_op jit(solution)/shard_map/while/body/eval_jaxpr/ppermute | solution.py:13
  52.4 20.1 %collective-permute-start = (bf16[4,512,64]{1,2,0:T(8,128)(2,1)S(1)}, bf16[4,512,64]{1,2,0:T(8,128)(2,1)S(1)}, u32[]{:S(2)}, u32[]{:S(2)}) collective-permute-start(bf16[4,512,64]{1,2,0:T(8,128)(2,1)S(1)} %copy.57), channel_id=1, source_target_pairs={{6,0},{0,2},{2,4},{4,6},{7,1},{1,3},{3,5},{5,7},{14,8},{8,10},{10,... | collective-permute-start | bytes 786440 | tf_op jit(solution)/shard_map/while/body/eval_jaxpr/ppermute | solution.py:13
  54.0 18.5 %collective-permute-start.1 = (f32[4,512]{1,0:T(4,128)S(1)}, f32[4,512]{1,0:T(4,128)S(1)}, u32[]{:S(2)}, u32[]{:S(2)}) collective-permute-start(f32[4,512]{1,0:T(4,128)S(1)} %max.12), channel_id=1, source_target_pairs={{6,0},{0,2},{2,4},{4,6},{7,1},{1,3},{3,5},{5,7},{14,8},{8,10},{10,... | collective-permute-start | bytes 24584 | tf_op jit(solution)/shard_map/while/body/eval_jaxpr/ppermute | solution.py:13
  55.6 17.0 %collective-permute-start.2 = (f32[4,512]{1,0:T(4,128)S(1)}, f32[4,512]{1,0:T(4,128)S(1)}, u32[]{:S(2)}, u32[]{:S(2)}) collective-permute-start(f32[4,512]{1,0:T(4,128)S(1)} %get-tuple-element.440), channel_id=1, source_target_pairs={{6,0},{0,2},{2,4},{4,6},{7,1},{1,3},{3,5},{5,7},{14,8},{8,10},{10,... | collective-permute-start | bytes 24584 | tf_op jit(solution)/shard_map/while/body/eval_jaxpr/ppermute | solution.py:13
  102.8 21.1 %collective-permute-start.3 = (f32[4,512,64]{1,2,0:T(8,128)}, f32[4,512,64]{1,2,0:T(8,128)S(1)}, u32[]{:S(2)}, u32[]{:S(2)}) collective-permute-start(f32[4,512,64]{1,2,0:T(8,128)} %fusion.89), channel_id=1, source_target_pairs={{6,0},{0,2},{2,4},{4,6},{7,1},{1,3},{3,5},{5,7},{14,8},{8,10},{10,... | collective-permute-start | bytes 1572872 | tf_op jit(solution)/shard_map/while/body/eval_jaxpr/ppermute | solution.py:13
  102.8 21.1 %collective-permute-start = (bf16[4,512,64]{1,2,0:T(8,128)(2,1)S(1)}, bf16[4,512,64]{1,2,0:T(8,128)(2,1)S(1)}, u32[]{:S(2)}, u32[]{:S(2)}) collective-permute-start(bf16[4,512,64]{1,2,0:T(8,128)(2,1)S(1)} %copy.57), channel_id=1, source_target_pairs={{6,0},{0,2},{2,4},{4,6},{7,1},{1,3},{3,5},{5,7},{14,8},{8,10},{10,... | collective-permute-start | bytes 786440 | tf_op jit(solution)/shard_map/while/body/eval_jaxpr/ppermute | solution.py:13
  104.1 19.7 %collective-permute-start.1 = (f32[4,512]{1,0:T(4,128)S(1)}, f32[4,512]{1,0:T(4,128)S(1)}, u32[]{:S(2)}, u32[]{:S(2)}) collective-permute-start(f32[4,512]{1,0:T(4,128)S(1)} %max.12), channel_id=1, source_target_pairs={{6,0},{0,2},{2,4},{4,6},{7,1},{1,3},{3,5},{5,7},{14,8},{8,10},{10,... | collective-permute-start | bytes 24584 | tf_op jit(solution)/shard_map/while/body/eval_jaxpr/ppermute | solution.py:13
  105.7 18.2 %collective-permute-start.2 = (f32[4,512]{1,0:T(4,128)S(1)}, f32[4,512]{1,0:T(4,128)S(1)}, u32[]{:S(2)}, u32[]{:S(2)}) collective-permute-start(f32[4,512]{1,0:T(4,128)S(1)} %get-tuple-element.440), channel_id=1, source_target_pairs={{6,0},{0,2},{2,4},{4,6},{7,1},{1,3},{3,5},{5,7},{14,8},{8,10},{10,... | collective-permute-start | bytes 24584 | tf_op jit(solution)/shard_map/while/body/eval_jaxpr/ppermute | solution.py:13
  154.1 20.2 %collective-permute-start.3 = (f32[4,512,64]{1,2,0:T(8,128)}, f32[4,512,64]{1,2,0:T(8,128)S(1)}, u32[]{:S(2)}, u32[]{:S(2)}) collective-permute-start(f32[4,512,64]{1,2,0:T(8,128)} %fusion.89), channel_id=1, source_target_pairs={{6,0},{0,2},{2,4},{4,6},{7,1},{1,3},{3,5},{5,7},{14,8},{8,10},{10,... | collective-permute-start | bytes 1572872 | tf_op jit(solution)/shard_map/while/body/eval_jaxpr/ppermute | solution.py:13
  154.1 20.2 %collective-permute-start = (bf16[4,512,64]{1,2,0:T(8,128)(2,1)S(1)}, bf16[4,512,64]{1,2,0:T(8,128)(2,1)S(1)}, u32[]{:S(2)}, u32[]{:S(2)}) collective-permute-start(bf16[4,512,64]{1,2,0:T(8,128)(2,1)S(1)} %copy.57), channel_id=1, source_target_pairs={{6,0},{0,2},{2,4},{4,6},{7,1},{1,3},{3,5},{5,7},{14,8},{8,10},{10,... | collective-permute-start | bytes 786440 | tf_op jit(solution)/shard_map/while/body/eval_jaxpr/ppermute | solution.py:13
  154.1 20.1 %collective-permute-start.1 = (f32[4,512]{1,0:T(4,128)S(1)}, f32[4,512]{1,0:T(4,128)S(1)}, u32[]{:S(2)}, u32[]{:S(2)}) collective-permute-start(f32[4,512]{1,0:T(4,128)S(1)} %max.12), channel_id=1, source_target_pairs={{6,0},{0,2},{2,4},{4,6},{7,1},{1,3},{3,5},{5,7},{14,8},{8,10},{10,... | collective-permute-start | bytes 24584 | tf_op jit(solution)/shard_map/while/body/eval_jaxpr/ppermute | solution.py:13
  154.9 19.4 %collective-permute-start.2 = (f32[4,512]{1,0:T(4,128)S(1)}, f32[4,512]{1,0:T(4,128)S(1)}, u32[]{:S(2)}, u32[]{:S(2)}) collective-permute-start(f32[4,512]{1,0:T(4,128)S(1)} %get-tuple-element.440), channel_id=1, source_target_pairs={{6,0},{0,2},{2,4},{4,6},{7,1},{1,3},{3,5},{5,7},{14,8},{8,10},{10,... | collective-permute-start | bytes 24584 | tf_op jit(solution)/shard_map/while/body/eval_jaxpr/ppermute | solution.py:13
  204.6 19.4 %collective-permute-start.3 = (f32[4,512,64]{1,2,0:T(8,128)}, f32[4,512,64]{1,2,0:T(8,128)S(1)}, u32[]{:S(2)}, u32[]{:S(2)}) collective-permute-start(f32[4,512,64]{1,2,0:T(8,128)} %fusion.89), channel_id=1, source_target_pairs={{6,0},{0,2},{2,4},{4,6},{7,1},{1,3},{3,5},{5,7},{14,8},{8,10},{10,... | collective-permute-start | bytes 1572872 | tf_op jit(solution)/shard_map/while/body/eval_jaxpr/ppermute | solution.py:13
  204.6 19.4 %collective-permute-start = (bf16[4,512,64]{1,2,0:T(8,128)(2,1)S(1)}, bf16[4,512,64]{1,2,0:T(8,128)(2,1)S(1)}, u32[]{:S(2)}, u32[]{:S(2)}) collective-permute-start(bf16[4,512,64]{1,2,0:T(8,128)(2,1)S(1)} %copy.57), channel_id=1, source_target_pairs={{6,0},{0,2},{2,4},{4,6},{7,1},{1,3},{3,5},{5,7},{14,8},{8,10},{10,... | collective-permute-start | bytes 786440 | tf_op jit(solution)/shard_map/while/body/eval_jaxpr/ppermute | solution.py:13
  204.6 19.3 %collective-permute-start.1 = (f32[4,512]{1,0:T(4,128)S(1)}, f32[4,512]{1,0:T(4,128)S(1)}, u32[]{:S(2)}, u32[]{:S(2)}) collective-permute-start(f32[4,512]{1,0:T(4,128)S(1)} %max.12), channel_id=1, source_target_pairs={{6,0},{0,2},{2,4},{4,6},{7,1},{1,3},{3,5},{5,7},{14,8},{8,10},{10,... | collective-permute-start | bytes 24584 | tf_op jit(solution)/shard_map/while/body/eval_jaxpr/ppermute | solution.py:13
  205.3 18.7 %collective-permute-start.2 = (f32[4,512]{1,0:T(4,128)S(1)}, f32[4,512]{1,0:T(4,128)S(1)}, u32[]{:S(2)}, u32[]{:S(2)}) collective-permute-start(f32[4,512]{1,0:T(4,128)S(1)} %get-tuple-element.440), channel_id=1, source_target_pairs={{6,0},{0,2},{2,4},{4,6},{7,1},{1,3},{3,5},{5,7},{14,8},{8,10},{10,... | collective-permute-start | bytes 24584 | tf_op jit(solution)/shard_map/while/body/eval_jaxpr/ppermute | solution.py:13
  225.4 8.9 %copy-start.4 = (s32[1,64,4]{1,2,0:T(4,128)S(1)}, s32[1,64,4]{1,2,0:T(4,128)}, u32[]{:S(2)}) copy-start(s32[1,64,4]{1,2,0:T(4,128)} %param.23) | copy-start | bytes 3076
  225.4 31.9 %copy-start = (bf16[1,64,2880]{2,1,0:T(8,128)(2,1)S(1)}, bf16[1,64,2880]{2,1,0:T(8,128)(2,1)}, u32[]{:S(2)}) copy-start(bf16[1,64,2880]{2,1,0:T(8,128)(2,1)} %param.15) | copy-start | bytes 1105924
  234.2 25.2 %copy-start.3 = (f32[2880]{0:T(1024)S(1)}, f32[2880]{0:T(1024)}, u32[]{:S(2)}) copy-start(f32[2880]{0:T(1024)} %param.22) | copy-start | bytes 34564
  234.2 115.1 %reduce-scatter.2.cloned.1.call-start = ((), (), s32[]{:S(2)}) async-start(), calls=%async_computation.4 | async-start | bytes 2211840 | tf_op jit(solution)/shard_map/reduce_scatter | solution.py:118
  326.3 30.9 %copy-start.5 = (f32[1,64,4]{1,2,0:T(4,128)S(1)}, f32[1,64,4]{1,2,0:T(4,128)}, u32[]{:S(2)}) copy-start(f32[1,64,4]{1,2,0:T(4,128)} %param.24) | copy-start | bytes 3076
  326.3 52.2 %copy-start.1 = (f32[64,2880]{1,0:T(8,128)S(1)}, f32[64,2880]{1,0:T(8,128)}, u32[]{:S(2)}) copy-start(f32[64,2880]{1,0:T(8,128)} %get-tuple-element.355) | copy-start | bytes 2211844
  351.6 26.8 %all-to-all-start.1 = ((bf16[1440,16,16]{0,2,1:T(8,128)(2,1)}), bf16[1440,16,16]{0,2,1:T(8,128)(2,1)S(1)}, u32[]{:S(2)}, u32[]{:S(2)}) async-start(bf16[1440,16,16]{0,2,1:T(8,128)(2,1)} %bitcast.20), calls=%async_computation.2 | async-start | bytes 1572864 | tf_op jit(solution)/shard_map/all_to_all | solution.py:126
Sparse Core Ops, SparseCore 0:
  234.3 22.8 all-reduce.1
  326.4 22.8 reduce-scatter.1
where the time goes:
time: 387 us; the launch traced here: 386 us
  waiting for transfers between devices  128 us (33%)
  matrix products  118 us (30%)
  other arithmetic  49.5 us (13%)
  blocking collectives  42.1 us (11%)
  starting transfers between devices  26.7 us (7%)
  between operations  13.6 us (4%)
  local copies, waits for them, and re-layouts  8.03 us (2%)
    ppermute x16, waiting for transfers between devices, passed_along(): return lax.ppermute(block, axis, route)  62.7 us
    dot_general x4, matrix products, absorb(): jnp.einsum('hrk,hkd->hrd', weights.astype(jnp.bfloat16), values, preferre...  46.3 us
    all_to_all x1, blocking collectives, body(): lax.all_to_all(packed, ('seq', 'ctx'), split_axis=0, concat_axis=0, tiled...  42.1 us
    reduce_sum x4, other arithmetic, absorb(): total = total * fade + jnp.sum(weights, axis=-1)  38.2 us
    dot_general x4, matrix products, absorb(): jnp.einsum('hrd,hkd->hrk', block, keys, preferred_element_type=jnp.float32)  30.9 us
    reduce_scatter x1, waiting for transfers between devices, body(): lax.psum_scatter(jnp.einsum('fd,rf->dr', columns, hidden, preferred_eleme...  23 us
    psum x1, waiting for transfers between devices, body(): lax.psum(projected.astype(jnp.bfloat16), 'head').astype(jnp.float32)  21.4 us
    ppermute x16, starting transfers between devices, passed_along(): return lax.ppermute(block, axis, route)  21.1 us
  transfers between devices with their start and end apart: 19, of which 11 were waited for; matrix products, arithmetic and copies ran while one was open for 0% of the time, Pallas kernels for 0%

commit v1 on v0

--- a/solution.py
+++ b/solution.py
@@ -123,7 +123,15 @@
         scatter_dimension=0,
         tiled=True,
     )
-    returned = lax.all_to_all(expert_out, ("seq", "ctx"), split_axis=1, concat_axis=1, tiled=True)
+    returned = jnp.concatenate(
+        lax.all_to_all(
+            jnp.stack(jnp.split(expert_out, lax.axis_size(("seq", "ctx")), axis=1)),
+            ("seq", "ctx"),
+            0,
+            0,
+        ),
+        axis=1,
+    )
     spread_weights = jnp.where(matches.T, expert_weights[0].reshape(-1)[:, None], 0.0)
     spread_weights = jnp.sum(spread_weights.reshape(count, -1, slots), axis=1)
     moe = lax.dot_general(

time: 387 us -> 417 us (1.078)
  local copies, waits for them, and re-layouts: 8.03 us -> 37 us
    another operation x1 -> x19, local copies, waits for them, and re-layouts: 0.01 us -> 18.8 us  [the longest x18 18.8 us: body(): jnp.stack(jnp.split(expert_out, lax.axis_size(('seq', 'ctx')), axis=1))]
    unnamed x16 -> x31, local copies, waits for them, and re-layouts: 2.6 us -> 15.1 us
where the time goes in v1:
time: 417 us; the launch traced here: 415 us
  waiting for transfers between devices  128 us (31%)
  matrix products  118 us (28%)
  other arithmetic  49.5 us (12%)
  blocking collectives  42.1 us (10%)
  local copies, waits for them, and re-layouts  37 us (9%)
  starting transfers between devices  26.7 us (6%)
  between operations  13.7 us (3%)
    ppermute x16, waiting for transfers between devices, passed_along(): return lax.ppermute(block, axis, route)  62.7 us
    dot_general x4, matrix products, absorb(): jnp.einsum('hrk,hkd->hrd', weights.astype(jnp.bfloat16), values, preferre...  46.3 us
    all_to_all x1, blocking collectives, body(): lax.all_to_all(packed, ('seq', 'ctx'), split_axis=0, concat_axis=0, tiled...  42.1 us
    reduce_sum x4, other arithmetic, absorb(): total = total * fade + jnp.sum(weights, axis=-1)  38.2 us
    dot_general x4, matrix products, absorb(): jnp.einsum('hrd,hkd->hrk', block, keys, preferred_element_type=jnp.float32)  30.9 us
    reduce_scatter x1, waiting for transfers between devices, body(): lax.psum_scatter(jnp.einsum('fd,rf->dr', columns, hidden, preferred_eleme...  23 us
    psum x1, waiting for transfers between devices, body(): lax.psum(projected.astype(jnp.bfloat16), 'head').astype(jnp.float32)  21.4 us
    ppermute x16, starting transfers between devices, passed_along(): return lax.ppermute(block, axis, route)  21.1 us
  transfers between devices with their start and end apart: 19, of which 11 were waited for; matrix products, arithmetic and copies ran while one was open for 0% of the time, Pallas kernels for 0%

profile of v1, /device:TPU:0, one launch (start us, length us, event | category | flops | bytes accessed | tf_op | source)
XLA Modules:
  0.0 415.5 jit_solution(11660024576236889951)
XLA Ops:
  8.5 6.7 %fusion.43 = bf16[64,2048]{1,0:T(8,128)(2,1)S(1)} fusion(bf16[2880,2048]{1,0:T(8,128)(2,1)} %param.16, bf16[1,64,2880]{2,1,0:T(8,128)(2,1)} %param.15), kind=kOutput, calls=%fused_computation.38 | convolution fusion | flops 755105792 | bytes 12427264 | tf_op jit(solution)/shard_map/dot_general | solution.py:42
  16.4 2.4 maximum_bitcast_fusion
  18.9 205.2 %while.22 = (s32[]{:T(128)}, bf16[4,512,64]{1,2,0:T(8,128)(2,1)S(1)}, f32[4,512]{1,0:T(4,128)S(1)}, f32[4,512]{1,0:T(4,128)S(1)}, f32[4,512,64]{1,2,0:T(8,128)S(...) while((s32[]{:T(128)}, ...), condition=%wide.region_3.4_spmd.clone, body=%wide.region_0.3_spmd.clone.sunk | while | flops 1161629696 | bytes 63567040 | solution.py:82
  19.1 1.3 fusion.86
  20.5 7.7 %fusion.87 = (f32[4,512]{1,0:T(4,128)S(1)}, f32[4,512,2112]{1,2,0:T(8,128)}) fusion(pred[512,2112]{0,1:T(8,128)(4,1)S(1)} %fusion.86, bf16[4,512,64]{1,2,0:T(8,128)(2,1)S(1)} %copy.100, bf16[4,2112,64]{1,2,0:T(8,128)(2,1)S(1)} %get-tuple-element.508), kind=kOutput, calls=%fused_computation.4.clone.1 | convolution fusion | flops 566622208 | bytes 19734528 | tf_op jit(solution)/shard_map/while/body/eval_jaxpr/hrd,hkd->hrk/dot_general | solution.py:66
  28.2 9.6 %fusion.88 = f32[4,512]{1,0:T(4,128)S(1)} fusion(f32[4,512,2112]{1,2,0:T(8,128)} %get-tuple-element.467, f32[4,512]{1,0:T(4,128)S(1)} %max.12, pred[512,2112]{0,1:T(8,128)(4,1)S(1)} %fusion.86), kind=kLoop, calls=%fused_computation.6.clone.1 | loop fusion | flops 17299456 | bytes 18399232 | tf_op jit(solution)/shard_map/while/body/eval_jaxpr/reduce_sum | solution.py:71
  37.8 11.6 %fusion.89 = f32[4,512,64]{1,2,0:T(8,128)} fusion(bf16[4,2112,64]{1,2,0:T(8,128)(2,1)} %get-tuple-element.509, f32[4,512,2112]{1,2,0:T(8,128)} %get-tuple-element.467, f32[4,512]{1,0:T(4,128)S(1)} %max.12, pred[512,2112]{0,1:T(8,128)(4,1)S(1)} %fusion.86, f32[4,512,64]{1,2,0:T(8,128)S(1)} %get-tuple-element.490, f32[4,512]{1,0:T(4,128)S(1)} %get-tuple-element.469), kind=kOutput, calls=%fused_computation.15.clone.1 | convolution fusion | flops 571211776 | bytes 20529152 | tf_op jit(solution)/shard_map/while/body/eval_jaxpr/hrk,hkd->hrd/dot_general | solution.py:72
  49.4 3.1 collective-permute-start.3
  52.4 1.6 collective-permute-start
  54.0 1.6 collective-permute-start.1
  55.6 16.9 %collective-permute-done.1 = f32[4,512]{1,0:T(4,128)S(1)} collective-permute-done((f32[4,512]{1,0:T(4,128)S(1)}, f32[4,512]{1,0:T(4,128)S(1)}, u32[]{:S(2)}, u32[]{:S(2)}) %collective-permute-start.1) | collective-permute-done | bytes 8224 | tf_op jit(solution)/shard_map/while/body/eval_jaxpr/ppermute | solution.py:13
  72.6 1.3 fusion.86
  73.9 7.7 %fusion.87 = (f32[4,512]{1,0:T(4,128)S(1)}, f32[4,512,2112]{1,2,0:T(8,128)}) fusion(pred[512,2112]{0,1:T(8,128)(4,1)S(1)} %fusion.86, bf16[4,512,64]{1,2,0:T(8,128)(2,1)S(1)} %copy.100, bf16[4,2112,64]{1,2,0:T(8,128)(2,1)S(1)} %get-tuple-element.508), kind=kOutput, calls=%fused_computation.4.clone.1 | convolution fusion | flops 566622208 | bytes 19734528 | tf_op jit(solution)/shard_map/while/body/eval_jaxpr/hrd,hkd->hrk/dot_general | solution.py:66
  81.6 9.6 %fusion.88 = f32[4,512]{1,0:T(4,128)S(1)} fusion(f32[4,512,2112]{1,2,0:T(8,128)} %get-tuple-element.467, f32[4,512]{1,0:T(4,128)S(1)} %max.12, pred[512,2112]{0,1:T(8,128)(4,1)S(1)} %fusion.86), kind=kLoop, calls=%fused_computation.6.clone.1 | loop fusion | flops 17299456 | bytes 18399232 | tf_op jit(solution)/shard_map/while/body/eval_jaxpr/reduce_sum | solution.py:71
  91.2 11.6 %fusion.89 = f32[4,512,64]{1,2,0:T(8,128)} fusion(bf16[4,2112,64]{1,2,0:T(8,128)(2,1)} %get-tuple-element.509, f32[4,512,2112]{1,2,0:T(8,128)} %get-tuple-element.467, f32[4,512]{1,0:T(4,128)S(1)} %max.12, pred[512,2112]{0,1:T(8,128)(4,1)S(1)} %fusion.86, f32[4,512,64]{1,2,0:T(8,128)S(1)} %get-tuple-element.490, f32[4,512]{1,0:T(4,128)S(1)} %get-tuple-element.469), kind=kOutput, calls=%fused_computation.15.clone.1 | convolution fusion | flops 571211776 | bytes 20529152 | tf_op jit(solution)/shard_map/while/body/eval_jaxpr/hrk,hkd->hrd/dot_general | solution.py:72
  104.1 1.6 collective-permute-start.1
  105.7 2.1 collective-permute-start.2
  107.8 16.0 %collective-permute-done.1 = f32[4,512]{1,0:T(4,128)S(1)} collective-permute-done((f32[4,512]{1,0:T(4,128)S(1)}, f32[4,512]{1,0:T(4,128)S(1)}, u32[]{:S(2)}, u32[]{:S(2)}) %collective-permute-start.1) | collective-permute-done | bytes 8224 | tf_op jit(solution)/shard_map/while/body/eval_jaxpr/ppermute | solution.py:13
  123.9 1.3 fusion.86
  125.2 7.7 %fusion.87 = (f32[4,512]{1,0:T(4,128)S(1)}, f32[4,512,2112]{1,2,0:T(8,128)}) fusion(pred[512,2112]{0,1:T(8,128)(4,1)S(1)} %fusion.86, bf16[4,512,64]{1,2,0:T(8,128)(2,1)S(1)} %copy.100, bf16[4,2112,64]{1,2,0:T(8,128)(2,1)S(1)} %get-tuple-element.508), kind=kOutput, calls=%fused_computation.4.clone.1 | convolution fusion | flops 566622208 | bytes 19734528 | tf_op jit(solution)/shard_map/while/body/eval_jaxpr/hrd,hkd->hrk/dot_general | solution.py:66
  133.0 9.6 %fusion.88 = f32[4,512]{1,0:T(4,128)S(1)} fusion(f32[4,512,2112]{1,2,0:T(8,128)} %get-tuple-element.467, f32[4,512]{1,0:T(4,128)S(1)} %max.12, pred[512,2112]{0,1:T(8,128)(4,1)S(1)} %fusion.86), kind=kLoop, calls=%fused_computation.6.clone.1 | loop fusion | flops 17299456 | bytes 18399232 | tf_op jit(solution)/shard_map/while/body/eval_jaxpr/reduce_sum | solution.py:71
  142.5 11.6 %fusion.89 = f32[4,512,64]{1,2,0:T(8,128)} fusion(bf16[4,2112,64]{1,2,0:T(8,128)(2,1)} %get-tuple-element.509, f32[4,512,2112]{1,2,0:T(8,128)} %get-tuple-element.467, f32[4,512]{1,0:T(4,128)S(1)} %max.12, pred[512,2112]{0,1:T(8,128)(4,1)S(1)} %fusion.86, f32[4,512,64]{1,2,0:T(8,128)S(1)} %get-tuple-element.490, f32[4,512]{1,0:T(4,128)S(1)} %get-tuple-element.469), kind=kOutput, calls=%fused_computation.15.clone.1 | convolution fusion | flops 571211776 | bytes 20529152 | tf_op jit(solution)/shard_map/while/body/eval_jaxpr/hrk,hkd->hrd/dot_general | solution.py:72
  154.9 4.2 %collective-permute-start.2 = (f32[4,512]{1,0:T(4,128)S(1)}, f32[4,512]{1,0:T(4,128)S(1)}, u32[]{:S(2)}, u32[]{:S(2)}) collective-permute-start(f32[4,512]{1,0:T(4,128)S(1)} %get-tuple-element.468), channel_id=1, source_target_pairs={{6,0},{0,2},{2,4},{4,6},{7,1},{1,3},{3,5},{5,7},{14,8},{8,10},{10,... | collective-permute-start | bytes 24584 | tf_op jit(solution)/shard_map/while/body/eval_jaxpr/ppermute | solution.py:13
  159.1 15.2 %collective-permute-done.1 = f32[4,512]{1,0:T(4,128)S(1)} collective-permute-done((f32[4,512]{1,0:T(4,128)S(1)}, f32[4,512]{1,0:T(4,128)S(1)}, u32[]{:S(2)}, u32[]{:S(2)}) %collective-permute-start.1) | collective-permute-done | bytes 8224 | tf_op jit(solution)/shard_map/while/body/eval_jaxpr/ppermute | solution.py:13
  175.7 7.7 %fusion.87 = (f32[4,512]{1,0:T(4,128)S(1)}, f32[4,512,2112]{1,2,0:T(8,128)}) fusion(pred[512,2112]{0,1:T(8,128)(4,1)S(1)} %fusion.86, bf16[4,512,64]{1,2,0:T(8,128)(2,1)S(1)} %copy.100, bf16[4,2112,64]{1,2,0:T(8,128)(2,1)S(1)} %get-tuple-element.508), kind=kOutput, calls=%fused_computation.4.clone.1 | convolution fusion | flops 566622208 | bytes 19734528 | tf_op jit(solution)/shard_map/while/body/eval_jaxpr/hrd,hkd->hrk/dot_general | solution.py:66
  183.4 9.6 %fusion.88 = f32[4,512]{1,0:T(4,128)S(1)} fusion(f32[4,512,2112]{1,2,0:T(8,128)} %get-tuple-element.467, f32[4,512]{1,0:T(4,128)S(1)} %max.12, pred[512,2112]{0,1:T(8,128)(4,1)S(1)} %fusion.86), kind=kLoop, calls=%fused_computation.6.clone.1 | loop fusion | flops 17299456 | bytes 18399232 | tf_op jit(solution)/shard_map/while/body/eval_jaxpr/reduce_sum | solution.py:71
  193.0 11.6 %fusion.89 = f32[4,512,64]{1,2,0:T(8,128)} fusion(bf16[4,2112,64]{1,2,0:T(8,128)(2,1)} %get-tuple-element.509, f32[4,512,2112]{1,2,0:T(8,128)} %get-tuple-element.467, f32[4,512]{1,0:T(4,128)S(1)} %max.12, pred[512,2112]{0,1:T(8,128)(4,1)S(1)} %fusion.86, f32[4,512,64]{1,2,0:T(8,128)S(1)} %get-tuple-element.490, f32[4,512]{1,0:T(4,128)S(1)} %get-tuple-element.469), kind=kOutput, calls=%fused_computation.15.clone.1 | convolution fusion | flops 571211776 | bytes 20529152 | tf_op jit(solution)/shard_map/while/body/eval_jaxpr/hrk,hkd->hrd/dot_general | solution.py:72
  205.3 4.3 %collective-permute-start.2 = (f32[4,512]{1,0:T(4,128)S(1)}, f32[4,512]{1,0:T(4,128)S(1)}, u32[]{:S(2)}, u32[]{:S(2)}) collective-permute-start(f32[4,512]{1,0:T(4,128)S(1)} %get-tuple-element.468), channel_id=1, source_target_pairs={{6,0},{0,2},{2,4},{4,6},{7,1},{1,3},{3,5},{5,7},{14,8},{8,10},{10,... | collective-permute-start | bytes 24584 | tf_op jit(solution)/shard_map/while/body/eval_jaxpr/ppermute | solution.py:13
  209.5 14.3 %collective-permute-done.1 = f32[4,512]{1,0:T(4,128)S(1)} collective-permute-done((f32[4,512]{1,0:T(4,128)S(1)}, f32[4,512]{1,0:T(4,128)S(1)}, u32[]{:S(2)}, u32[]{:S(2)}) %collective-permute-start.1) | collective-permute-done | bytes 8224 | tf_op jit(solution)/shard_map/while/body/eval_jaxpr/ppermute | solution.py:13
  225.4 8.8 %convolution_convert_fusion.1 = bf16[64,2880]{1,0:T(8,128)(2,1)} fusion(bf16[64,2048]{1,0:T(8,128)(2,1)S(1)} %reshape.176, bf16[2048,2880]{0,1:T(8,128)(2,1)} %param.21), kind=kOutput, calls=%fused_computation.31 | convolution fusion | flops 755159040 | bytes 12427264 | tf_op jit(solution)/shard_map/dot_general | solution.py:90
  235.8 21.4 %all-reduce.2.cloned.1.call-done = bf16[64,2880]{1,0:T(8,128)(2,1)} async-done(((bf16[64,2880]{1,0:T(8,128)(2,1)}), bf16[64,2880]{1,0:T(8,128)(2,1)}) %all-reduce.2.cloned.1.call-update) | async-done | bytes 368656 | tf_op jit(solution)/shard_map/psum | solution.py:93
  257.3 2.1 convert_add_fusion
  259.4 1.7 convolution_convert_fusion
  262.1 42.1 %all_to_all.10 = bf16[16,16,2880]{2,1,0:T(8,128)(2,1)S(1)} all-to-all(bf16[16,16,2880]{2,1,0:T(8,128)(2,1)S(1)} %bitcast.135), channel_id=1, replica_groups=mesh['seq'=4,'ctx'=4,'head'=2] {'seq','ctx'}, dimensions={0} | all-to-all | bytes 2949120 | tf_op jit(solution)/shard_map/all_to_all | solution.py:112
  304.1 5.9 %fusion.25 = f32[256,1440]{0,1:T(8,128)S(1)} fusion(bf16[256,2880]{1,0:T(8,128)(2,1)S(1)} %bitcast.138, bf16[1,2880,1440]{1,2,0:T(8,128)(2,1)} %param.25), kind=kOutput, calls=%fused_computation.26 | convolution fusion | flops 2123366400 | bytes 11243520 | tf_op jit(solution)/shard_map/dot_general | solution.py:114
  310.0 16.2 %fusion.30 = bf16[2880,256]{1,0:T(8,128)(2,1)} fusion(bf16[1,1440,2880]{2,1,0:T(8,128)(2,1)} %param.27, bf16[256,2880]{1,0:T(8,128)(2,1)S(1)} %bitcast.139, bf16[1,2880,1440]{1,2,0:T(8,128)(2,1)} %param.26, f32[256,1440]{0,1:T(8,128)S(1)} %fusion.25), kind=kOutput, calls=%fused_computation.30 | convolution fusion | flops 4250419200 | bytes 21012480 | tf_op jit(solution)/shard_map/fd,rf->dr/dot_general | solution.py:119
  326.3 23.0 %reduce-scatter.2.cloned.1.call-done = bf16[1440,256]{1,0:T(8,128)(2,1)} async-done(((bf16[2880,256]{1,0:T(8,128)(2,1)}), bf16[1440,256]{1,0:T(8,128)(2,1)}) %reduce-scatter.2.cloned.1.call-update) | async-done | bytes 737296 | tf_op jit(solution)/shard_map/reduce_scatter | solution.py:118
  349.3 6.4 %slice_bitcast_fusion = (bf16[1,1440,16]{2,1,0:T(8,128)(2,1)S(1)}, bf16[1,1440,16]{2,1,0:T(8,128)(2,1)S(1)}, bf16[1,1440,16]{2,1,0:T(8,128)(2,1)S(1)}, bf16[1,14...) fusion(bf16[1440,256]{1,0:T(8,128)(2,1)} %reduce-scatter.2.clon, ...), kind=kLoop, calls=%fused_computation.53 | loop fusion | bytes 1474560 | tf_op jit(solution)/shard_map/stack | solution.py:128
  357.5 1.7 copy.75
  359.2 1.7 copy.76
  361.0 1.7 copy.77
  362.7 1.7 copy.78
  368.1 1.4 constant_dynamic-update-slice_fusion.14
  369.5 1.4 constant_dynamic-update-slice_fusion.13
  371.0 1.4 constant_dynamic-update-slice_fusion.12
  372.4 1.4 constant_dynamic-update-slice_fusion.11
  380.6 5.6 %all-to-all-start.1 = ((bf16[16,1440,16]{1,2,0:T(8,128)(2,1)}), bf16[16,1440,16]{1,2,0:T(8,128)(2,1)S(1)}, u32[]{:S(2)}, u32[]{:S(2)}) async-start(bf16[16,1440,16]{1,2,0:T(8,128)(2,1)} %constant_dynamic-update-slice_fusion), calls=%async_computation.2 | async-start | bytes 1572864 | tf_op jit(solution)/shard_map/all_to_all | solution.py:127
  386.3 21.1 %all-to-all-done.1 = bf16[16,1440,16]{1,2,0:T(8,128)(2,1)S(1)} async-done(((bf16[16,1440,16]{1,2,0:T(8,128)(2,1)}), bf16[16,1440,16]{1,2,0:T(8,128)(2,1)S(1)}, u32[]{:S(2)}, u32[]{:S(2)}) %all-to-all-start.1) | async-done | bytes 737312 | tf_op jit(solution)/shard_map/all_to_all | solution.py:127
  (106 shorter events, 25.1 us)
Async XLA Ops:
  6.5 250.7 %all-reduce.2.cloned.1.call-start = ((), (), s32[]{:S(2)}) async-start(), calls=%async_computation.3 | async-start | bytes 753664 | tf_op jit(solution)/shard_map/psum | solution.py:93
  15.2 1.2 copy-start.2
  49.4 23.2 %collective-permute-start.3 = (f32[4,512,64]{1,2,0:T(8,128)}, f32[4,512,64]{1,2,0:T(8,128)S(1)}, u32[]{:S(2)}, u32[]{:S(2)}) collective-permute-start(f32[4,512,64]{1,2,0:T(8,128)} %fusion.89), channel_id=1, source_target_pairs={{6,0},{0,2},{2,4},{4,6},{7,1},{1,3},{3,5},{5,7},{14,8},{8,10},{10,... | collective-permute-start | bytes 1572872 | tf_op jit(solution)/shard_map/while/body/eval_jaxpr/ppermute | solution.py:13
  52.4 20.1 %collective-permute-start = (bf16[4,512,64]{1,2,0:T(8,128)(2,1)S(1)}, bf16[4,512,64]{1,2,0:T(8,128)(2,1)S(1)}, u32[]{:S(2)}, u32[]{:S(2)}) collective-permute-start(bf16[4,512,64]{1,2,0:T(8,128)(2,1)S(1)} %copy.100), channel_id=1, source_target_pairs={{6,0},{0,2},{2,4},{4,6},{7,1},{1,3},{3,5},{5,7},{14,8},{8,10},{10,... | collective-permute-start | bytes 786440 | tf_op jit(solution)/shard_map/while/body/eval_jaxpr/ppermute | solution.py:13
  54.0 18.5 %collective-permute-start.1 = (f32[4,512]{1,0:T(4,128)S(1)}, f32[4,512]{1,0:T(4,128)S(1)}, u32[]{:S(2)}, u32[]{:S(2)}) collective-permute-start(f32[4,512]{1,0:T(4,128)S(1)} %max.12), channel_id=1, source_target_pairs={{6,0},{0,2},{2,4},{4,6},{7,1},{1,3},{3,5},{5,7},{14,8},{8,10},{10,... | collective-permute-start | bytes 24584 | tf_op jit(solution)/shard_map/while/body/eval_jaxpr/ppermute | solution.py:13
  55.6 17.0 %collective-permute-start.2 = (f32[4,512]{1,0:T(4,128)S(1)}, f32[4,512]{1,0:T(4,128)S(1)}, u32[]{:S(2)}, u32[]{:S(2)}) collective-permute-start(f32[4,512]{1,0:T(4,128)S(1)} %get-tuple-element.468), channel_id=1, source_target_pairs={{6,0},{0,2},{2,4},{4,6},{7,1},{1,3},{3,5},{5,7},{14,8},{8,10},{10,... | collective-permute-start | bytes 24584 | tf_op jit(solution)/shard_map/while/body/eval_jaxpr/ppermute | solution.py:13
  102.8 21.1 %collective-permute-start.3 = (f32[4,512,64]{1,2,0:T(8,128)}, f32[4,512,64]{1,2,0:T(8,128)S(1)}, u32[]{:S(2)}, u32[]{:S(2)}) collective-permute-start(f32[4,512,64]{1,2,0:T(8,128)} %fusion.89), channel_id=1, source_target_pairs={{6,0},{0,2},{2,4},{4,6},{7,1},{1,3},{3,5},{5,7},{14,8},{8,10},{10,... | collective-permute-start | bytes 1572872 | tf_op jit(solution)/shard_map/while/body/eval_jaxpr/ppermute | solution.py:13
  102.8 21.1 %collective-permute-start = (bf16[4,512,64]{1,2,0:T(8,128)(2,1)S(1)}, bf16[4,512,64]{1,2,0:T(8,128)(2,1)S(1)}, u32[]{:S(2)}, u32[]{:S(2)}) collective-permute-start(bf16[4,512,64]{1,2,0:T(8,128)(2,1)S(1)} %copy.100), channel_id=1, source_target_pairs={{6,0},{0,2},{2,4},{4,6},{7,1},{1,3},{3,5},{5,7},{14,8},{8,10},{10,... | collective-permute-start | bytes 786440 | tf_op jit(solution)/shard_map/while/body/eval_jaxpr/ppermute | solution.py:13
  104.1 19.7 %collective-permute-start.1 = (f32[4,512]{1,0:T(4,128)S(1)}, f32[4,512]{1,0:T(4,128)S(1)}, u32[]{:S(2)}, u32[]{:S(2)}) collective-permute-start(f32[4,512]{1,0:T(4,128)S(1)} %max.12), channel_id=1, source_target_pairs={{6,0},{0,2},{2,4},{4,6},{7,1},{1,3},{3,5},{5,7},{14,8},{8,10},{10,... | collective-permute-start | bytes 24584 | tf_op jit(solution)/shard_map/while/body/eval_jaxpr/ppermute | solution.py:13
  105.7 18.2 %collective-permute-start.2 = (f32[4,512]{1,0:T(4,128)S(1)}, f32[4,512]{1,0:T(4,128)S(1)}, u32[]{:S(2)}, u32[]{:S(2)}) collective-permute-start(f32[4,512]{1,0:T(4,128)S(1)} %get-tuple-element.468), channel_id=1, source_target_pairs={{6,0},{0,2},{2,4},{4,6},{7,1},{1,3},{3,5},{5,7},{14,8},{8,10},{10,... | collective-permute-start | bytes 24584 | tf_op jit(solution)/shard_map/while/body/eval_jaxpr/ppermute | solution.py:13
  154.1 20.2 %collective-permute-start.3 = (f32[4,512,64]{1,2,0:T(8,128)}, f32[4,512,64]{1,2,0:T(8,128)S(1)}, u32[]{:S(2)}, u32[]{:S(2)}) collective-permute-start(f32[4,512,64]{1,2,0:T(8,128)} %fusion.89), channel_id=1, source_target_pairs={{6,0},{0,2},{2,4},{4,6},{7,1},{1,3},{3,5},{5,7},{14,8},{8,10},{10,... | collective-permute-start | bytes 1572872 | tf_op jit(solution)/shard_map/while/body/eval_jaxpr/ppermute | solution.py:13
  154.1 20.2 %collective-permute-start = (bf16[4,512,64]{1,2,0:T(8,128)(2,1)S(1)}, bf16[4,512,64]{1,2,0:T(8,128)(2,1)S(1)}, u32[]{:S(2)}, u32[]{:S(2)}) collective-permute-start(bf16[4,512,64]{1,2,0:T(8,128)(2,1)S(1)} %copy.100), channel_id=1, source_target_pairs={{6,0},{0,2},{2,4},{4,6},{7,1},{1,3},{3,5},{5,7},{14,8},{8,10},{10,... | collective-permute-start | bytes 786440 | tf_op jit(solution)/shard_map/while/body/eval_jaxpr/ppermute | solution.py:13
  154.1 20.1 %collective-permute-start.1 = (f32[4,512]{1,0:T(4,128)S(1)}, f32[4,512]{1,0:T(4,128)S(1)}, u32[]{:S(2)}, u32[]{:S(2)}) collective-permute-start(f32[4,512]{1,0:T(4,128)S(1)} %max.12), channel_id=1, source_target_pairs={{6,0},{0,2},{2,4},{4,6},{7,1},{1,3},{3,5},{5,7},{14,8},{8,10},{10,... | collective-permute-start | bytes 24584 | tf_op jit(solution)/shard_map/while/body/eval_jaxpr/ppermute | solution.py:13
  154.9 19.4 %collective-permute-start.2 = (f32[4,512]{1,0:T(4,128)S(1)}, f32[4,512]{1,0:T(4,128)S(1)}, u32[]{:S(2)}, u32[]{:S(2)}) collective-permute-start(f32[4,512]{1,0:T(4,128)S(1)} %get-tuple-element.468), channel_id=1, source_target_pairs={{6,0},{0,2},{2,4},{4,6},{7,1},{1,3},{3,5},{5,7},{14,8},{8,10},{10,... | collective-permute-start | bytes 24584 | tf_op jit(solution)/shard_map/while/body/eval_jaxpr/ppermute | solution.py:13
  204.6 19.4 %collective-permute-start.3 = (f32[4,512,64]{1,2,0:T(8,128)}, f32[4,512,64]{1,2,0:T(8,128)S(1)}, u32[]{:S(2)}, u32[]{:S(2)}) collective-permute-start(f32[4,512,64]{1,2,0:T(8,128)} %fusion.89), channel_id=1, source_target_pairs={{6,0},{0,2},{2,4},{4,6},{7,1},{1,3},{3,5},{5,7},{14,8},{8,10},{10,... | collective-permute-start | bytes 1572872 | tf_op jit(solution)/shard_map/while/body/eval_jaxpr/ppermute | solution.py:13
  204.6 19.4 %collective-permute-start = (bf16[4,512,64]{1,2,0:T(8,128)(2,1)S(1)}, bf16[4,512,64]{1,2,0:T(8,128)(2,1)S(1)}, u32[]{:S(2)}, u32[]{:S(2)}) collective-permute-start(bf16[4,512,64]{1,2,0:T(8,128)(2,1)S(1)} %copy.100), channel_id=1, source_target_pairs={{6,0},{0,2},{2,4},{4,6},{7,1},{1,3},{3,5},{5,7},{14,8},{8,10},{10,... | collective-permute-start | bytes 786440 | tf_op jit(solution)/shard_map/while/body/eval_jaxpr/ppermute | solution.py:13
  204.6 19.3 %collective-permute-start.1 = (f32[4,512]{1,0:T(4,128)S(1)}, f32[4,512]{1,0:T(4,128)S(1)}, u32[]{:S(2)}, u32[]{:S(2)}) collective-permute-start(f32[4,512]{1,0:T(4,128)S(1)} %max.12), channel_id=1, source_target_pairs={{6,0},{0,2},{2,4},{4,6},{7,1},{1,3},{3,5},{5,7},{14,8},{8,10},{10,... | collective-permute-start | bytes 24584 | tf_op jit(solution)/shard_map/while/body/eval_jaxpr/ppermute | solution.py:13
  205.3 18.7 %collective-permute-start.2 = (f32[4,512]{1,0:T(4,128)S(1)}, f32[4,512]{1,0:T(4,128)S(1)}, u32[]{:S(2)}, u32[]{:S(2)}) collective-permute-start(f32[4,512]{1,0:T(4,128)S(1)} %get-tuple-element.468), channel_id=1, source_target_pairs={{6,0},{0,2},{2,4},{4,6},{7,1},{1,3},{3,5},{5,7},{14,8},{8,10},{10,... | collective-permute-start | bytes 24584 | tf_op jit(solution)/shard_map/while/body/eval_jaxpr/ppermute | solution.py:13
  225.4 8.9 %copy-start.4 = (s32[1,64,4]{1,2,0:T(4,128)S(1)}, s32[1,64,4]{1,2,0:T(4,128)}, u32[]{:S(2)}) copy-start(s32[1,64,4]{1,2,0:T(4,128)} %param.23) | copy-start | bytes 3076
  225.4 31.9 %copy-start = (bf16[1,64,2880]{2,1,0:T(8,128)(2,1)S(1)}, bf16[1,64,2880]{2,1,0:T(8,128)(2,1)}, u32[]{:S(2)}) copy-start(bf16[1,64,2880]{2,1,0:T(8,128)(2,1)} %param.15) | copy-start | bytes 1105924
  234.2 25.2 %copy-start.3 = (f32[2880]{0:T(1024)S(1)}, f32[2880]{0:T(1024)}, u32[]{:S(2)}) copy-start(f32[2880]{0:T(1024)} %param.22) | copy-start | bytes 34564
  234.2 115.1 %reduce-scatter.2.cloned.1.call-start = ((), (), s32[]{:S(2)}) async-start(), calls=%async_computation.4 | async-start | bytes 2211840 | tf_op jit(solution)/shard_map/reduce_scatter | solution.py:118
  367.7 18.5 %copy-start.5 = (f32[1,64,4]{1,2,0:T(4,128)S(1)}, f32[1,64,4]{1,2,0:T(4,128)}, u32[]{:S(2)}) copy-start(f32[1,64,4]{1,2,0:T(4,128)} %param.24) | copy-start | bytes 3076
  367.7 39.8 %copy-start.1 = (f32[64,2880]{1,0:T(8,128)S(1)}, f32[64,2880]{1,0:T(8,128)}, u32[]{:S(2)}) copy-start(f32[64,2880]{1,0:T(8,128)} %get-tuple-element.367) | copy-start | bytes 2211844
  380.6 26.8 %all-to-all-start.1 = ((bf16[16,1440,16]{1,2,0:T(8,128)(2,1)}), bf16[16,1440,16]{1,2,0:T(8,128)(2,1)S(1)}, u32[]{:S(2)}, u32[]{:S(2)}) async-start(bf16[16,1440,16]{1,2,0:T(8,128)(2,1)} %constant_dynamic-update-slice_fusion), calls=%async_computation.2 | async-start | bytes 1572864 | tf_op jit(solution)/shard_map/all_to_all | solution.py:127
Sparse Core Ops, SparseCore 0:
  234.3 22.8 all-reduce.1
  326.4 22.8 reduce-scatter.1
